TPU v7x, 32 devices: a whole 2x2x4 slice. The times are simulated.
32 devices in a mesh: dp: 4 (over z), expert: 8 (over y, x, core).
Axes of the slice: x: 2, y: 2, z: 4, core: 2. Of those that a mesh axis runs over, the one named last changes fastest.
Arguments:
- tokens: bfloat16 [32, 212, 1024], P(('dp', 'expert')), may hold values from -6 to 6
- expert_ids: int32 [32, 212, 1], P(('dp', 'expert')), may hold values from 0 to 7; in each aligned block of 212 rows (0 to 211, 212 to 423, ..., all dimensions but the last counted through in order) at most 36 rows name the same one
- caption_lengths: int32 [32], P(('dp', 'expert')), may hold values from 1 to 16, as said below
- layer_norm_gain: float32 [1024], replicated, may hold values from 0.5 to 1.5
- router: float32 [1024, 8], replicated, may hold values from -0.1875 to 0.1875
- w_up: bfloat16 [8, 1024, 4096], P('expert', None, 'dp'), may hold values from -0.1875 to 0.1875
- w_down: bfloat16 [8, 4096, 1024], P('expert', 'dp'), may hold values from -0.09375 to 0.09375
- logit_scale: float32 [1], replicated, may hold values from 5 to 20
- logit_bias: float32 [1], replicated, may hold values from -4 to -1.5
Outputs:
- loss: float32 [1], replicated
- grad_tokens: bfloat16 [32, 212, 1024], P(('dp', 'expert'))
- grad_up: float32 [8, 1024, 4096], P('expert', None, 'dp')
- grad_down: float32 [8, 4096, 1024], P('expert', 'dp')
- grad_router: float32 [1024, 8], replicated
- layer_gain_gradient: float32 [1024], replicated
Inputs may be any that keep to these rules, and one draw needn't show every extreme that they name: `expert_ids`: among the rows of one device (aligned blocks of 212 rows, devices ordered by dp then expert) no expert is named more than 36 times, a bound that some block reaches. `caption_lengths`: some caption has all 16 tokens.
All inputs are finite; a program needn't handle non-finite values.
Results may differ from a plain program's by a relative error of at most 0.009.
Values may be sent and summed in bfloat16 or wider, within the bound.
A program may use at most 128 MiB of HBM per device.

v0:
```python
import jax
import jax.numpy as jnp
from jax import lax
from jax.sharding import PartitionSpec as P

D = 1024
PATCH = 196
CAPLEN = 16
SEQ = 212
eps = 1e-06
loss_scale = 1024.0


def gelu_slope(pre):
    return (
        0.5 * (1.0 + lax.erf(pre * 0.7071067811865476))
        + pre * jnp.exp(-0.5 * pre * pre) * 0.3989422804014327
    )


def deliver(buffer, experts, slots):
    width = buffer.shape[-1]
    sent = lax.all_to_all(
        buffer.reshape(experts, 1, slots, width), "expert", split_axis=0, concat_axis=1, tiled=True
    )
    shaped = sent.reshape(sent.shape[0], 1, sent.shape[1], slots, width)
    whole = lax.all_gather(shaped, "dp", axis=1, tiled=True)
    return whole.reshape(whole.shape[0], -1, width)


def give_back(partial_value, n_dp, n_expert, slots):
    local = partial_value.shape[0]
    width = partial_value.shape[-1]
    summed = lax.psum_scatter(
        partial_value.reshape(local, n_dp, n_expert * slots, width).astype(jnp.bfloat16),
        "dp",
        scatter_dimension=1,
        tiled=True,
    )
    rounded = summed.reshape(local, n_expert, slots, width)
    returned = lax.all_to_all(rounded, "expert", split_axis=1, concat_axis=0, tiled=True)
    return returned.reshape(-1, width)


def body(
    tokens,
    expert_ids,
    caption_lengths,
    layer_norm_gain,
    router,
    w_up,
    w_down,
    logit_scale,
    logit_bias,
):
    n_dp = lax.axis_size("dp")
    n_expert = lax.axis_size("expert")
    pair_dev = tokens.shape[0]
    rows = pair_dev * SEQ
    experts = router.shape[1]
    slots = rows * 4 // (3 * experts) + 1
    pairs_all = pair_dev * n_dp * n_expert
    input_rows = tokens.reshape(rows, D).astype(jnp.float32)
    input_mean = jnp.mean(input_rows, axis=1, keepdims=True)
    var_x = jnp.mean((input_rows - input_mean) ** 2, axis=1, keepdims=True)
    inverse_deviation = 1.0 / jnp.sqrt(var_x + eps)
    centered_scaled_input = (input_rows - input_mean) * inverse_deviation
    normalized_input = (centered_scaled_input * layer_norm_gain).astype(jnp.bfloat16)
    ids = expert_ids.reshape(rows)
    onehot = (ids[:, None] == jnp.arange(experts, dtype=jnp.int32)[None, :]).astype(jnp.int32)
    slot = jnp.sum((jnp.cumsum(onehot, axis=0) - 1) * onehot, axis=1)
    dest = ids * slots + slot
    onehot_f = onehot.astype(jnp.float32)
    buffer = jnp.zeros((experts * slots, D), jnp.bfloat16).at[dest].set(normalized_input)
    gathered = deliver(buffer, experts, slots)
    pre = jnp.einsum("erd,edf->erf", gathered, w_up, preferred_element_type=jnp.float32)
    act = jax.nn.gelu(pre, approximate=False).astype(jnp.bfloat16)
    partial_value = jnp.einsum("erf,efd->erd", act, w_down, preferred_element_type=jnp.float32)
    moe = give_back(partial_value, n_dp, n_expert, slots)[dest].astype(jnp.float32)
    xnf = normalized_input.astype(jnp.float32)
    router_logits = jnp.dot(xnf, router, precision=lax.Precision.HIGHEST)
    gate = jax.nn.sigmoid(jnp.sum(router_logits * onehot_f, axis=1))
    y = (input_rows + gate[:, None] * moe).reshape(pair_dev, SEQ, D)
    img = jnp.mean(y[:, :PATCH], axis=1)
    lengths = caption_lengths.astype(jnp.float32)
    mask = (jnp.arange(CAPLEN, dtype=jnp.int32)[None, :] < caption_lengths[:, None]).astype(
        jnp.float32
    )
    txt = jnp.sum(y[:, PATCH:] * mask[:, :, None], axis=1) / lengths[:, None]
    ru = jnp.sqrt(jnp.mean(img * img, axis=1, keepdims=True) + eps)
    rv = jnp.sqrt(jnp.mean(txt * txt, axis=1, keepdims=True) + eps)
    u = img / ru
    v = txt / rv
    scale = logit_scale[0]
    first = lax.axis_index(("dp", "expert")) * pair_dev
    mine = first + jnp.arange(pair_dev, dtype=jnp.int32)
    every = jnp.arange(pairs_all, dtype=jnp.int32)
    own_sign = jnp.where(mine[:, None] == every[None, :], 1.0, -1.0)
    u_all, v_all = (
        lax.all_gather(u, ("dp", "expert"), axis=0, tiled=True),
        lax.all_gather(v, ("dp", "expert"), axis=0, tiled=True),
    )
    logits = scale * jnp.dot(u, v_all.T, precision=lax.Precision.HIGHEST) / D + logit_bias[0]
    loss_term = -jnp.sum(jax.nn.log_sigmoid(own_sign * logits)) / pairs_all
    coef = -(loss_scale / pairs_all) * own_sign * jax.nn.sigmoid(-own_sign * logits)
    du = scale / D * jnp.dot(coef, v_all, precision=lax.Precision.HIGHEST)
    column_logits = scale * jnp.dot(u_all, v.T, precision=lax.Precision.HIGHEST) / D + logit_bias[0]
    column_sign = own_sign.T
    column_coef = (
        -(loss_scale / pairs_all) * column_sign * jax.nn.sigmoid(-column_sign * column_logits)
    )
    dv = scale / D * jnp.dot(column_coef.T, u_all, precision=lax.Precision.HIGHEST)
    dimg = (du - u * jnp.mean(du * u, axis=1, keepdims=True)) / ru
    dtxt = (dv - v * jnp.mean(dv * v, axis=1, keepdims=True)) / rv
    dy_img = jnp.broadcast_to(dimg[:, None, :] / PATCH, (pair_dev, PATCH, D))
    dy_txt = (dtxt / lengths[:, None])[:, None, :] * mask[:, :, None]
    dy = jnp.concatenate([dy_img, dy_txt], axis=1).reshape(rows, D)
    dmoe = (gate[:, None] * dy).astype(jnp.bfloat16)
    dgl = jnp.sum(dy * moe, axis=1) * gate * (1.0 - gate)
    router_part = jnp.dot(xnf.T, onehot_f * dgl[:, None], precision=lax.Precision.HIGHEST)
    grad_buffer = jnp.zeros((experts * slots, D), jnp.bfloat16).at[dest].set(dmoe)
    gathered_grads = deliver(grad_buffer, experts, slots)
    dact = jnp.einsum("erd,efd->erf", gathered_grads, w_down, preferred_element_type=jnp.float32)
    dpre = (dact * gelu_slope(pre)).astype(jnp.bfloat16)
    grad_down = jnp.einsum("erf,erd->efd", act, gathered_grads, preferred_element_type=jnp.float32)
    grad_up = jnp.einsum("erd,erf->edf", gathered, dpre, preferred_element_type=jnp.float32)
    back_partial = jnp.einsum("erf,edf->erd", dpre, w_up, preferred_element_type=jnp.float32)
    dxe = give_back(back_partial, n_dp, n_expert, slots)[dest].astype(jnp.float32)
    router_rows = jnp.dot(onehot_f, router.T, precision=lax.Precision.HIGHEST)
    gradient_normalized_input = dxe + dgl[:, None] * router_rows
    gain_partial_term = jnp.sum(gradient_normalized_input * centered_scaled_input, axis=0)
    scaled_output_gradient = gradient_normalized_input * layer_norm_gain
    normed_input_gradient = (
        scaled_output_gradient
        - jnp.mean(scaled_output_gradient, axis=1, keepdims=True)
        - centered_scaled_input
        * jnp.mean(scaled_output_gradient * centered_scaled_input, axis=1, keepdims=True)
    ) * inverse_deviation
    grad_tokens = (dy + normed_input_gradient).astype(jnp.bfloat16).reshape(pair_dev, SEQ, D)
    loss, grad_router, layer_gain_gradient = lax.psum(
        (loss_term, router_part, gain_partial_term), ("dp", "expert")
    )
    return (loss.reshape(1), grad_tokens, grad_up, grad_down, grad_router, layer_gain_gradient)


def solution(mesh):
    return jax.shard_map(
        body,
        mesh=mesh,
        in_specs=(
            P(("dp", "expert"), None, None),
            P(("dp", "expert"), None, None),
            P(("dp", "expert")),
            P(),
            P(),
            P("expert", None, "dp"),
            P("expert", "dp", None),
            P(),
            P(),
        ),
        out_specs=(
            P(),
            P(("dp", "expert"), None, None),
            P("expert", None, "dp"),
            P("expert", "dp", None),
            P(),
            P(),
        ),
        check_vma=False,
    )
```

profile of v0, /device:TPU:0, one launch (start us, length us, event | category | flops | bytes accessed | tf_op | source)
XLA Modules:
  0.0 468.2 jit_solution(15633228378693927035)
XLA Ops:
  15.3 16.1 %all_to_all.16 = bf16[8,1,36,1024]{3,2,1,0:T(8,128)(2,1)S(1)} all-to-all(bf16[8,1,36,1024]{3,2,1,0:T(8,128)(2,1)S(1)} %bitcast.185), channel_id=1, replica_groups=mesh['dp'=4,'expert'=8] {'expert'}, dimensions={0} | all-to-all | bytes 1179648 | tf_op jit(solution)/shard_map/all_to_all | solution.py:23
  32.6 49.5 %all-gather.7.cloned.1.call-done = bf16[32,1,36,1024]{3,0,2,1:T(8,128)(2,1)} async-done(((bf16[8,1,36,1024]{3,0,2,1:T(8,128)(2,1)}), bf16[32,1,36,1024]{3,0,2,1:T(8,128)(2,1)}) %all-gather.7.cloned.1.call-update) | async-done | bytes 2359312 | tf_op jit(solution)/shard_map/all_gather | solution.py:27
  82.1 4.5 copy.17
  86.5 4.1 reshape.516
  90.7 14.6 %fusion.2 = (bf16[1152,1024]{1,0:T(8,128)(2,1)S(1)}, f32[1152,1024]{1,0:T(8,128)}) fusion(bf16[1152,1024]{1,0:T(8,128)(2,1)} %reshape.516, bf16[1,1024,1024]{2,1,0:T(8,128)(2,1)S(1)} %copy-done), kind=kOutput, calls=%fused_computation.9 | convolution fusion | flops 2492596224 | bytes 11534336 | tf_op jit(solution)/shard_map/erd,edf->erf/dot_general | solution.py:76
  106.7 3.8 convert_bitcast_fusion.1
  111.5 45.7 %reduce-scatter.3.cloned.1.call-done = bf16[1,1,288,1024]{3,2,1,0:T(8,128)(2,1)} async-done(((bf16[1,4,288,1024]{3,2,1,0:T(8,128)(2,1)}), bf16[1,1,288,1024]{3,2,1,0:T(8,128)(2,1)}) %reduce-scatter.3.cloned.1.call-update) | async-done | bytes 589840 | tf_op jit(solution)/shard_map/reduce_scatter | solution.py:34
  159.2 4.2 all-to-all-start.1
  165.3 9.2 %all-to-all-done.1 = bf16[1,8,36,1024]{3,2,0,1:T(8,128)(2,1)} async-done(((bf16[1,8,36,1024]{3,2,0,1:T(8,128)(2,1)}), bf16[1,8,36,1024]{3,2,0,1:T(8,128)(2,1)}, u32[]{:S(2)}, u32[]{:S(2)}) %all-to-all-start.1) | async-done | bytes 589856 | tf_op jit(solution)/shard_map/all_to_all | solution.py:41
  181.6 38.6 %all-gather.1 = f32[32768]{0:T(1024)S(1)} all-gather(f32[1024]{0:T(1024)S(1)} %broadcast_divide_fusion), channel_id=3, replica_groups=mesh['dp'=4,'expert'=8] {'dp','expert'}, dimensions={0}, use_global_device_ids=true | all-gather | bytes 135168 | tf_op jit(solution)/shard_map/all_gather | solution.py:101
  220.2 37.2 %all-gather.2 = f32[32768]{0:T(1024)S(1)} all-gather(f32[1024]{0:T(1024)S(1)} %multiply_divide_fusion), channel_id=4, replica_groups=mesh['dp'=4,'expert'=8] {'dp','expert'}, dimensions={0}, use_global_device_ids=true | all-gather | bytes 135168 | tf_op jit(solution)/shard_map/all_gather | solution.py:100
  266.0 14.6 %all_to_all.17 = bf16[8,1,36,1024]{3,2,1,0:T(8,128)(2,1)S(1)} all-to-all(bf16[8,1,36,1024]{3,2,1,0:T(8,128)(2,1)} %bitcast.186), channel_id=1, replica_groups=mesh['dp'=4,'expert'=8] {'expert'}, dimensions={0} | all-to-all | bytes 1179648 | tf_op jit(solution)/shard_map/all_to_all | solution.py:23
  281.8 46.4 %all-gather.9.cloned.1.call-done = bf16[32,1,36,1024]{3,0,2,1:T(8,128)(2,1)} async-done(((bf16[8,1,36,1024]{3,0,2,1:T(8,128)(2,1)}), bf16[32,1,36,1024]{3,0,2,1:T(8,128)(2,1)}) %all-gather.9.cloned.1.call-update) | async-done | bytes 2359312 | tf_op jit(solution)/shard_map/all_gather | solution.py:27
  328.2 4.5 copy.21
  332.7 4.1 reshape.525
  336.8 6.8 %fusion.14 = bf16[1152,1024]{1,0:T(8,128)(2,1)S(1)} fusion(f32[1152,1024]{1,0:T(8,128)} %get-tuple-element.13, bf16[1152,1024]{1,0:T(8,128)(2,1)} %reshape.525, bf16[1,1024,1024]{2,1,0:T(8,128)(2,1)} %param.15), kind=kOutput, calls=%fused_computation.29 | convolution fusion | flops 2427715584 | bytes 11534336 | tf_op jit(solution)/shard_map/erd,efd->erf/dot_general | solution.py:123
  345.0 3.9 convert_bitcast_fusion
  352.2 7.7 %convolution_bitcast_fusion = f32[1,1024,1024]{2,1,0:T(8,128)} fusion(bf16[1152,1024]{1,0:T(8,128)(2,1)} %copy-done.8, bf16[1152,1024]{1,0:T(8,128)(2,1)} %reshape.525), kind=kOutput, calls=%fused_computation.32 | convolution fusion | flops 2415919104 | bytes 8912896 | tf_op jit(solution)/shard_map/erf,erd->efd/dot_general | solution.py:125
  359.9 35.7 %reduce-scatter.5.cloned.1.call-done = bf16[1,1,288,1024]{3,2,1,0:T(8,128)(2,1)} async-done(((bf16[1,4,288,1024]{3,2,1,0:T(8,128)(2,1)}), bf16[1,1,288,1024]{3,2,1,0:T(8,128)(2,1)}) %reduce-scatter.5.cloned.1.call-update) | async-done | bytes 589840 | tf_op jit(solution)/shard_map/reduce_scatter | solution.py:34
  397.6 4.4 all-to-all-start.3
  402.0 7.3 %convolution_bitcast_fusion.1 = f32[1,1024,1024]{2,1,0:T(8,128)} fusion(bf16[1152,1024]{1,0:T(8,128)(2,1)} %reshape.516, bf16[1152,1024]{1,0:T(8,128)(2,1)} %copy-done.9), kind=kOutput, calls=%fused_computation.33 | convolution fusion | flops 2415919104 | bytes 8912896 | tf_op jit(solution)/shard_map/erd,erf->edf/dot_general | solution.py:126
  409.4 3.6 all-to-all-done.3
  416.0 3.1 fusion.56
  419.1 40.1 %all-reduce.1 = (f32[1]{0:T(128)}, f32[1024,8]{0,1:T(8,128)}, f32[1024]{0:T(1024)}) all-reduce(f32[1]{0:T(128)} %bitcast.22, f32[1024,8]{0,1:T(8,128)S(1)} %fusion.70, f32[1024]{0:T(1024)S(1)} %get-tuple-element.6), channel_id=1, replica_groups=mesh['dp'=4,'expert'=8] {'dp','expert'}, use_global_device_ids=true, to_apply=%region_13.14 | all-reduce | flops 9217 | bytes 73736 | tf_op jit(solution)/shard_map/psum | solution.py:140
  (82 shorter events, 39.1 us)
Async XLA Ops:
  7.2 83.5 %copy-start = (bf16[1,1024,1024]{2,1,0:T(8,128)(2,1)S(1)}, bf16[1,1024,1024]{2,1,0:T(8,128)(2,1)}, u32[]{:S(2)}) copy-start(bf16[1,1024,1024]{2,1,0:T(8,128)(2,1)} %param.14) | copy-start | bytes 6291460
  7.2 74.9 %all-gather.7.cloned.1.call-start = ((), (), s32[]{:S(2)}) async-start(), calls=%async_computation.8 | async-start | bytes 2949120 | tf_op jit(solution)/shard_map/all_gather | solution.py:27
  32.6 124.7 %reduce-scatter.3.cloned.1.call-start = ((), (), s32[]{:S(2)}) async-start(), calls=%async_computation.6 | async-start | bytes 2949120 | tf_op jit(solution)/shard_map/reduce_scatter | solution.py:34
  90.6 16.1 %copy-start.7 = (bf16[1,1024,1024]{2,1,0:T(8,128)(2,1)S(1)}, bf16[1,1024,1024]{2,1,0:T(8,128)(2,1)}, u32[]{:S(2)}) copy-start(bf16[1,1024,1024]{2,1,0:T(8,128)(2,1)} %param.15) | copy-start | bytes 6291460
  105.3 1.5 copy-start.8
  106.7 4.5 copy-start.1
  106.7 4.5 copy-start.4
  110.6 54.3 %copy-start.5 = (f32[1024,8]{0,1:T(8,128)S(1)}, f32[1024,8]{0,1:T(8,128)}, u32[]{:S(2)}) copy-start(f32[1024,8]{0,1:T(8,128)} %param.13) | copy-start | bytes 98308
  110.6 54.3 %copy-start.6 = (s32[1,212,1]{1,2,0:T(1,128)S(1)}, s32[1,212,1]{1,2,0:T(1,128)}, u32[]{:S(2)}) copy-start(s32[1,212,1]{1,2,0:T(1,128)} %param.10) | copy-start | bytes 2548
  111.5 53.8 %copy-start.3 = (bf16[212,1024]{1,0:T(8,128)(2,1)}, bf16[212,1024]{1,0:T(8,128)(2,1)S(1)}, u32[]{:S(2)}) copy-start(bf16[212,1024]{1,0:T(8,128)(2,1)S(1)} %fusion.50) | copy-start | bytes 1302532
  159.2 15.3 %all-to-all-start.1 = ((bf16[1,8,36,1024]{3,2,0,1:T(8,128)(2,1)}), bf16[1,8,36,1024]{3,2,0,1:T(8,128)(2,1)}, u32[]{:S(2)}, u32[]{:S(2)}) async-start(bf16[1,8,36,1024]{3,2,0,1:T(8,128)(2,1)} %bitcast.184), calls=%async_computation.2 | async-start | bytes 1310720 | tf_op jit(solution)/shard_map/all_to_all | solution.py:41
  163.4 164.8 %all-gather.9.cloned.1.call-start = ((), (), s32[]{:S(2)}) async-start(), calls=%async_computation.9 | async-start | bytes 2949120 | tf_op jit(solution)/shard_map/all_gather | solution.py:27
  261.6 88.0 %copy-start.2 = (f32[1,196,1024]{2,1,0:T(8,128)}, f32[1,196,1024]{2,1,0:T(8,128)S(1)}, u32[]{:S(2)}) copy-start(f32[1,196,1024]{2,1,0:T(8,128)S(1)} %broadcast_in_dim.10) | copy-start | bytes 2408452
  281.8 113.9 %reduce-scatter.5.cloned.1.call-start = ((), (), s32[]{:S(2)}) async-start(), calls=%async_computation.7 | async-start | bytes 2949120 | tf_op jit(solution)/shard_map/reduce_scatter | solution.py:34
  343.6 1.4 copy-start.9
  397.6 15.3 %all-to-all-start.3 = ((bf16[1,8,36,1024]{3,2,0,1:T(8,128)(2,1)}), bf16[1,8,36,1024]{3,2,0,1:T(8,128)(2,1)}, u32[]{:S(2)}, u32[]{:S(2)}) async-start(bf16[1,8,36,1024]{3,2,0,1:T(8,128)(2,1)} %bitcast.34), calls=%async_computation.5 | async-start | bytes 1310720 | tf_op jit(solution)/shard_map/all_to_all | solution.py:41
Sparse Core Ops, SparseCore 0:
  32.7 49.3 all-gather.6
  110.7 46.4 reduce-scatter.2
  281.9 46.2 all-gather.8
  349.1 46.4 reduce-scatter.4
where the time goes:
time: 470 us; the launch traced here: 468 us
  waiting for transfers between devices  190 us (40%)
  blocking collectives  147 us (31%)
  matrix products  50.6 us (11%)
  local copies, waits for them, and re-layouts  34.9 us (7%)
  between operations  19.4 us (4%)
  other arithmetic  18 us (4%)
  starting transfers between devices  8.79 us (2%)
    all_gather x2, waiting for transfers between devices, deliver(): whole = lax.all_gather(shaped, 'dp', axis=1, tiled=True)  95.9 us
    reduce_scatter x2, waiting for transfers between devices, give_back(): lax.psum_scatter(partial_value.reshape(local, n_dp, n_expert * slots, wid...  81.4 us
    psum x1, blocking collectives, body(): lax.psum((loss_term, router_part, gain_partial_term), ('dp', 'expert'))  40.1 us
    all_gather x1, blocking collectives, body(): lax.all_gather(v, ('dp', 'expert'), axis=0, tiled=True)  38.6 us
    all_gather x1, blocking collectives, body(): lax.all_gather(u, ('dp', 'expert'), axis=0, tiled=True)  37.2 us
    all_to_all x2, blocking collectives, deliver(): lax.all_to_all(buffer.reshape(experts, 1, slots, width), 'expert', split_...  30.7 us
    dot_general x1, matrix products, body(): jnp.einsum('erd,edf->erf', gathered, w_up, preferred_element_type=jnp.flo...  14.6 us
    all_to_all x2, waiting for transfers between devices, give_back(): lax.all_to_all(rounded, 'expert', split_axis=1, concat_axis=0, tiled=True)  12.8 us
  transfers between devices with their start and end apart: 6, of which 6 were waited for; matrix products, arithmetic and copies ran while one was open for 4% of the time, Pallas kernels for 0%

commit v1 on v0

--- a/solution.py
+++ b/solution.py
@@ -53,6 +53,12 @@
     logit_scale,
     logit_bias,
 ):
+
+    def do_loads(base_x):
+        piece_out = jnp.stack([base_x for _ in range(lax.axis_size(("dp", "expert")))], 0)
+        heard = lax.all_to_all(piece_out, ("dp", "expert"), 0, 0)
+        return jnp.concatenate(heard, 0)
+
     n_dp = lax.axis_size("dp")
     n_expert = lax.axis_size("expert")
     pair_dev = tokens.shape[0]
@@ -96,10 +102,7 @@
     mine = first + jnp.arange(pair_dev, dtype=jnp.int32)
     every = jnp.arange(pairs_all, dtype=jnp.int32)
     own_sign = jnp.where(mine[:, None] == every[None, :], 1.0, -1.0)
-    u_all, v_all = (
-        lax.all_gather(u, ("dp", "expert"), axis=0, tiled=True),
-        lax.all_gather(v, ("dp", "expert"), axis=0, tiled=True),
-    )
+    u_all, v_all = (do_loads(u), lax.all_gather(v, ("dp", "expert"), axis=0, tiled=True))
     logits = scale * jnp.dot(u, v_all.T, precision=lax.Precision.HIGHEST) / D + logit_bias[0]
     loss_term = -jnp.sum(jax.nn.log_sigmoid(own_sign * logits)) / pairs_all
     coef = -(loss_scale / pairs_all) * own_sign * jax.nn.sigmoid(-own_sign * logits)

time: 470 us -> 445 us (0.947)
  blocking collectives: 147 us -> 109 us
  waiting for transfers between devices: 190 us -> 198 us
    all_gather x1 -> x0, blocking collectives: 37.2 us -> none  [body(): lax.all_gather(u, ('dp', 'expert'), axis=0, tiled=True)]
    all_to_all x0 -> x1, waiting for transfers between devices: none -> 6.88 us  [do_loads(): heard = lax.all_to_all(piece_out, ('dp', 'expert'), 0, 0)]
  transfers between devices with their start and end apart: 6 -> 7, of which waited for: 6 -> 7; matrix products, arithmetic and copies ran while one was open for 4% -> 4% of each run, Pallas kernels for 0% -> 0%
where the time goes in v1:
time: 445 us; the launch traced here: 444 us
  waiting for transfers between devices  198 us (44%)
  blocking collectives  109 us (24%)
  matrix products  50.6 us (11%)
  local copies, waits for them, and re-layouts  36.6 us (8%)
  between operations  19.3 us (4%)
  other arithmetic  18.6 us (4%)
  starting transfers between devices  11.4 us (3%)
    all_gather x2, waiting for transfers between devices, deliver(): whole = lax.all_gather(shaped, 'dp', axis=1, tiled=True)  96.6 us
    reduce_scatter x2, waiting for transfers between devices, give_back(): lax.psum_scatter(partial_value.reshape(local, n_dp, n_expert * slots, wid...  81.4 us
    psum x1, blocking collectives, body(): lax.psum((loss_term, router_part, gain_partial_term), ('dp', 'expert'))  40.1 us
    all_gather x1, blocking collectives, body(): lax.all_gather(v, ('dp', 'expert'), axis=0, tiled=True)  38.8 us
    all_to_all x2, blocking collectives, deliver(): lax.all_to_all(buffer.reshape(experts, 1, slots, width), 'expert', split_...  30.7 us
    dot_general x1, matrix products, body(): jnp.einsum('erd,edf->erf', gathered, w_up, preferred_element_type=jnp.flo...  14.6 us
    all_to_all x2, waiting for transfers between devices, give_back(): lax.all_to_all(rounded, 'expert', split_axis=1, concat_axis=0, tiled=True)  12.9 us
    all_gather x2, local copies, waits for them, and re-layouts, deliver(): whole = lax.all_gather(shaped, 'dp', axis=1, tiled=True)  8.94 us
  transfers between devices with their start and end apart: 7, of which 7 were waited for; matrix products, arithmetic and copies ran while one was open for 4% of the time, Pallas kernels for 0%

profile of v1, /device:TPU:0, one launch (start us, length us, event | category | flops | bytes accessed | tf_op | source)
XLA Modules:
  0.0 443.8 jit_solution(13328622317405310590)
XLA Ops:
  17.0 16.1 %all_to_all.20 = bf16[8,1,36,1024]{3,2,1,0:T(8,128)(2,1)S(1)} all-to-all(bf16[8,1,36,1024]{3,2,1,0:T(8,128)(2,1)S(1)} %bitcast.188), channel_id=1, replica_groups=mesh['dp'=4,'expert'=8] {'expert'}, dimensions={0} | all-to-all | bytes 1179648 | tf_op jit(solution)/shard_map/all_to_all | solution.py:23
  34.3 49.5 %all-gather.6.cloned.1.call-done = bf16[32,1,36,1024]{3,0,2,1:T(8,128)(2,1)} async-done(((bf16[8,1,36,1024]{3,0,2,1:T(8,128)(2,1)}), bf16[32,1,36,1024]{3,0,2,1:T(8,128)(2,1)}) %all-gather.6.cloned.1.call-update) | async-done | bytes 2359312 | tf_op jit(solution)/shard_map/all_gather | solution.py:27
  83.8 4.5 %copy.17 = bf16[32,1,36,1024]{3,2,0,1:T(8,128)(2,1)} copy(bf16[32,1,36,1024]{3,0,2,1:T(8,128)(2,1)} %all-gather.6.cloned.1.call-done) | data formatting | bytes 4718592 | tf_op jit(solution)/shard_map/all_gather | solution.py:27
  88.2 4.1 reshape.512
  92.4 14.6 %fusion.2 = (bf16[1152,1024]{1,0:T(8,128)(2,1)S(1)}, f32[1152,1024]{1,0:T(8,128)}) fusion(bf16[1152,1024]{1,0:T(8,128)(2,1)} %reshape.512, bf16[1,1024,1024]{2,1,0:T(8,128)(2,1)S(1)} %copy-done), kind=kOutput, calls=%fused_computation.9 | convolution fusion | flops 2492596224 | bytes 11534336 | tf_op jit(solution)/shard_map/erd,edf->erf/dot_general | solution.py:82
  108.4 3.8 convert_bitcast_fusion.1
  113.2 45.7 %reduce-scatter.3.cloned.1.call-done = bf16[1,1,288,1024]{3,2,1,0:T(8,128)(2,1)} async-done(((bf16[1,4,288,1024]{3,2,1,0:T(8,128)(2,1)}), bf16[1,1,288,1024]{3,2,1,0:T(8,128)(2,1)}) %reduce-scatter.3.cloned.1.call-update) | async-done | bytes 589840 | tf_op jit(solution)/shard_map/reduce_scatter | solution.py:34
  160.9 4.2 all-to-all-start.1
  167.0 9.3 %all-to-all-done.1 = bf16[1,8,36,1024]{3,2,0,1:T(8,128)(2,1)} async-done(((bf16[1,8,36,1024]{3,2,0,1:T(8,128)(2,1)}), bf16[1,8,36,1024]{3,2,0,1:T(8,128)(2,1)}, u32[]{:S(2)}, u32[]{:S(2)}) %all-to-all-start.1) | async-done | bytes 589856 | tf_op jit(solution)/shard_map/all_to_all | solution.py:41
  183.3 38.8 %all-gather.1 = f32[32768]{0:T(1024)S(1)} all-gather(f32[1024]{0:T(1024)S(1)} %broadcast_divide_fusion), channel_id=3, replica_groups=mesh['dp'=4,'expert'=8] {'dp','expert'}, dimensions={0}, use_global_device_ids=true | all-gather | bytes 135168 | tf_op jit(solution)/shard_map/all_gather | solution.py:105
  227.8 6.9 %all-to-all-done.2 = f32[32,1,1024]{2,1,0:T(1,128)S(1)} async-done(((f32[32,1,1024]{2,1,0:T(1,128)}), f32[32,1,1024]{2,1,0:T(1,128)S(1)}, u32[]{:S(2)}, u32[]{:S(2)}) %all-to-all-start.2) | async-done | bytes 131104 | tf_op jit(solution)/shard_map/all_to_all | solution.py:59
  240.9 14.6 %all_to_all.42 = bf16[8,1,36,1024]{3,2,1,0:T(8,128)(2,1)S(1)} all-to-all(bf16[8,1,36,1024]{3,2,1,0:T(8,128)(2,1)} %bitcast.189), channel_id=1, replica_groups=mesh['dp'=4,'expert'=8] {'expert'}, dimensions={0} | all-to-all | bytes 1179648 | tf_op jit(solution)/shard_map/all_to_all | solution.py:23
  256.7 47.1 %all-gather.8.cloned.1.call-done = bf16[32,1,36,1024]{3,0,2,1:T(8,128)(2,1)} async-done(((bf16[8,1,36,1024]{3,0,2,1:T(8,128)(2,1)}), bf16[32,1,36,1024]{3,0,2,1:T(8,128)(2,1)}) %all-gather.8.cloned.1.call-update) | async-done | bytes 2359312 | tf_op jit(solution)/shard_map/all_gather | solution.py:27
  303.8 4.5 %copy.21 = bf16[32,1,36,1024]{3,2,0,1:T(8,128)(2,1)} copy(bf16[32,1,36,1024]{3,0,2,1:T(8,128)(2,1)} %all-gather.8.cloned.1.call-done) | data formatting | bytes 4718592 | tf_op jit(solution)/shard_map/all_gather | solution.py:27
  308.3 4.1 reshape.522
  312.4 6.8 %fusion.14 = bf16[1152,1024]{1,0:T(8,128)(2,1)S(1)} fusion(f32[1152,1024]{1,0:T(8,128)} %get-tuple-element.13, bf16[1152,1024]{1,0:T(8,128)(2,1)} %reshape.522, bf16[1,1024,1024]{2,1,0:T(8,128)(2,1)} %param.15), kind=kOutput, calls=%fused_computation.29 | convolution fusion | flops 2427715584 | bytes 11534336 | tf_op jit(solution)/shard_map/erd,efd->erf/dot_general | solution.py:126
  320.6 3.9 convert_bitcast_fusion
  327.8 7.7 %convolution_bitcast_fusion = f32[1,1024,1024]{2,1,0:T(8,128)} fusion(bf16[1152,1024]{1,0:T(8,128)(2,1)} %copy-done.8, bf16[1152,1024]{1,0:T(8,128)(2,1)} %reshape.522), kind=kOutput, calls=%fused_computation.32 | convolution fusion | flops 2415919104 | bytes 8912896 | tf_op jit(solution)/shard_map/erf,erd->efd/dot_general | solution.py:128
  335.5 35.7 %reduce-scatter.5.cloned.1.call-done = bf16[1,1,288,1024]{3,2,1,0:T(8,128)(2,1)} async-done(((bf16[1,4,288,1024]{3,2,1,0:T(8,128)(2,1)}), bf16[1,1,288,1024]{3,2,1,0:T(8,128)(2,1)}) %reduce-scatter.5.cloned.1.call-update) | async-done | bytes 589840 | tf_op jit(solution)/shard_map/reduce_scatter | solution.py:34
  373.2 4.4 all-to-all-start.4
  377.7 7.3 %convolution_bitcast_fusion.1 = f32[1,1024,1024]{2,1,0:T(8,128)} fusion(bf16[1152,1024]{1,0:T(8,128)(2,1)} %reshape.512, bf16[1152,1024]{1,0:T(8,128)(2,1)} %copy-done.9), kind=kOutput, calls=%fused_computation.33 | convolution fusion | flops 2415919104 | bytes 8912896 | tf_op jit(solution)/shard_map/erd,erf->edf/dot_general | solution.py:129
  385.0 3.6 all-to-all-done.4
  391.6 3.1 fusion.56
  394.7 40.1 %all-reduce.1 = (f32[1]{0:T(128)}, f32[1024,8]{0,1:T(8,128)}, f32[1024]{0:T(1024)}) all-reduce(f32[1]{0:T(128)} %bitcast.22, f32[1024,8]{0,1:T(8,128)S(1)} %fusion.75, f32[1024]{0:T(1024)S(1)} %get-tuple-element.6), channel_id=1, replica_groups=mesh['dp'=4,'expert'=8] {'dp','expert'}, use_global_device_ids=true, to_apply=%region_13.14 | all-reduce | flops 9217 | bytes 73736 | tf_op jit(solution)/shard_map/psum | solution.py:143
  (83 shorter events, 44.1 us)
Async XLA Ops:
  7.2 85.2 %copy-start = (bf16[1,1024,1024]{2,1,0:T(8,128)(2,1)S(1)}, bf16[1,1024,1024]{2,1,0:T(8,128)(2,1)}, u32[]{:S(2)}) copy-start(bf16[1,1024,1024]{2,1,0:T(8,128)(2,1)} %param.14) | copy-start | bytes 6291460
  7.2 76.6 %all-gather.6.cloned.1.call-start = ((), (), s32[]{:S(2)}) async-start(), calls=%async_computation.9 | async-start | bytes 2949120 | tf_op jit(solution)/shard_map/all_gather | solution.py:27
  34.3 124.7 %reduce-scatter.3.cloned.1.call-start = ((), (), s32[]{:S(2)}) async-start(), calls=%async_computation.7 | async-start | bytes 2949120 | tf_op jit(solution)/shard_map/reduce_scatter | solution.py:34
  92.4 16.1 %copy-start.7 = (bf16[1,1024,1024]{2,1,0:T(8,128)(2,1)S(1)}, bf16[1,1024,1024]{2,1,0:T(8,128)(2,1)}, u32[]{:S(2)}) copy-start(bf16[1,1024,1024]{2,1,0:T(8,128)(2,1)} %param.15) | copy-start | bytes 6291460
  107.0 1.5 copy-start.8
  108.4 4.5 %copy-start.1 = (bf16[1,212,1024]{2,1,0:T(8,128)(2,1)S(1)}, bf16[1,212,1024]{2,1,0:T(8,128)(2,1)}, u32[]{:S(2)}) copy-start(bf16[1,212,1024]{2,1,0:T(8,128)(2,1)} %param.9) | copy-start | bytes 1302532
  108.4 4.5 %copy-start.4 = (f32[1024]{0:T(1024)S(1)}, f32[1024]{0:T(1024)}, u32[]{:S(2)}) copy-start(f32[1024]{0:T(1024)} %param.12) | copy-start | bytes 12292
  112.3 54.2 %copy-start.5 = (f32[1024,8]{0,1:T(8,128)S(1)}, f32[1024,8]{0,1:T(8,128)}, u32[]{:S(2)}) copy-start(f32[1024,8]{0,1:T(8,128)} %param.13) | copy-start | bytes 98308
  112.3 54.2 %copy-start.6 = (s32[1,212,1]{1,2,0:T(1,128)S(1)}, s32[1,212,1]{1,2,0:T(1,128)}, u32[]{:S(2)}) copy-start(s32[1,212,1]{1,2,0:T(1,128)} %param.10) | copy-start | bytes 2548
  113.2 53.8 %copy-start.3 = (bf16[212,1024]{1,0:T(8,128)(2,1)}, bf16[212,1024]{1,0:T(8,128)(2,1)S(1)}, u32[]{:S(2)}) copy-start(bf16[212,1024]{1,0:T(8,128)(2,1)S(1)} %fusion.50) | copy-start | bytes 1302532
  160.9 15.3 %all-to-all-start.1 = ((bf16[1,8,36,1024]{3,2,0,1:T(8,128)(2,1)}), bf16[1,8,36,1024]{3,2,0,1:T(8,128)(2,1)}, u32[]{:S(2)}, u32[]{:S(2)}) async-start(bf16[1,8,36,1024]{3,2,0,1:T(8,128)(2,1)} %bitcast.187), calls=%async_computation.2 | async-start | bytes 1310720 | tf_op jit(solution)/shard_map/all_to_all | solution.py:41
  223.8 10.8 %all-to-all-start.2 = ((f32[32,1,1024]{2,1,0:T(1,128)}), f32[32,1,1024]{2,1,0:T(1,128)S(1)}, u32[]{:S(2)}, u32[]{:S(2)}) async-start(f32[32,1,1024]{2,1,0:T(1,128)} %stack.2), calls=%async_computation.3 | async-start | bytes 262144 | tf_op jit(solution)/shard_map/all_to_all | solution.py:59
  226.4 77.4 %all-gather.8.cloned.1.call-start = ((), (), s32[]{:S(2)}) async-start(), calls=%async_computation.10 | async-start | bytes 2949120 | tf_op jit(solution)/shard_map/all_gather | solution.py:27
  236.5 88.7 %copy-start.2 = (f32[1,196,1024]{2,1,0:T(8,128)}, f32[1,196,1024]{2,1,0:T(8,128)S(1)}, u32[]{:S(2)}) copy-start(f32[1,196,1024]{2,1,0:T(8,128)S(1)} %broadcast_in_dim.10) | copy-start | bytes 2408452
  256.7 114.6 %reduce-scatter.5.cloned.1.call-start = ((), (), s32[]{:S(2)}) async-start(), calls=%async_computation.8 | async-start | bytes 2949120 | tf_op jit(solution)/shard_map/reduce_scatter | solution.py:34
  319.2 1.4 copy-start.9
  373.2 15.3 %all-to-all-start.4 = ((bf16[1,8,36,1024]{3,2,0,1:T(8,128)(2,1)}), bf16[1,8,36,1024]{3,2,0,1:T(8,128)(2,1)}, u32[]{:S(2)}, u32[]{:S(2)}) async-start(bf16[1,8,36,1024]{3,2,0,1:T(8,128)(2,1)} %bitcast.34), calls=%async_computation.6 | async-start | bytes 1310720 | tf_op jit(solution)/shard_map/all_to_all | solution.py:41
Sparse Core Ops, SparseCore 0:
  34.4 49.3 all-gather.5
  112.4 46.4 reduce-scatter.2
  256.8 46.9 all-gather.7
  324.7 46.4 reduce-scatter.4
